TPU v7x, 128 devices: a whole 4x4x4 slice. The times are simulated.
128 devices in a mesh: prow: 4 (over x), pcol: 32 (over z, y, core).
Axes of the slice: x: 4, y: 4, z: 4, core: 2. Of those that a mesh axis runs over, the one named last changes fastest.
Arguments:
- match_tiles: float32 [128, 8, 128, 128], P('pcol', 'prow'), may hold values from 0.05 to 1
- pattern: int32 [128, 8], replicated, may hold values from 0 to 127, as said below
- kept: int32 [128, 8], replicated, may hold values from 0 to 127, as said below
- panel_order: int32 [32], replicated, may hold values from 0 to 31, as said below
Outputs:
- clusters: float32 [128, 8, 128, 128], P('pcol', 'prow')
Inputs may be any that keep to these rules, and one draw needn't show every extreme that they name: `pattern`: slots r * 2 to r * 2 + 1 of a tile column name 2 different tile rows of the r-th of the equal row blocks along prow. Tile column j names itself and tile column j + 1 - 2 * (j % 2) in the row block that holds tile row j. Of the tile columns of one panel, the tile columns of any other panel name at most 1 different ones, and exactly 1 for some pairs of panels. `kept`: as for pattern, with the same 1; every named tile is nonzero in the product of the input matrix with itself. `panel_order`: A permutation in which every entry differs from its index by at most one.
All inputs are finite; a program needn't handle non-finite values.
Results may differ from a plain program's by a relative error of at most 0.0003.
Values sent between devices are 32-bit elements; how exact they have to be, the bound alone decides.
No kernel may reach another device: no remote copies, remote signals or barrier semaphores. Data moves between devices by JAX's collectives and lax.ppermute only.
A program may use at most 64 MiB of HBM per device.

v0:
```python
import jax
import jax.numpy as jnp
from jax import lax
from jax.sharding import PartitionSpec as P


def copy_for_each(x, axis):
    length = lax.axis_size(axis)
    return lax.all_to_all(jnp.broadcast_to(x[None], (length, *x.shape)), axis, 0, 0, tiled=True)


def of_everyone(x, axis):
    everything = copy_for_each(x, axis)
    return jnp.sum(everything, axis=0)


def joined_along(tiles, dim):
    shape = list(tiles.shape[1:])
    shape[dim] *= tiles.shape[0]
    return jnp.moveaxis(tiles, 0, dim).reshape(shape)


def gather_directly(x, axis, dim):
    tiles = copy_for_each(x, axis)
    return joined_along(tiles, dim)


def column_partial(row_block):
    return jnp.sum(row_block, axis=(1, 2))


def sum_columns(partial_value):
    return of_everyone(partial_value, "prow")


def gather_pieces_together(row_block, want_whole):
    partial_value = column_partial(row_block)
    whole_cols = None
    totals = sum_columns(partial_value)
    normal = row_block / totals[:, None, None, :]
    if want_whole:
        whole_cols = gather_directly(normal, "prow", 1)
    return (whole_cols, normal)


def locate(column_ids, wanted):
    matches = column_ids[None, None, :] == wanted[:, :, None]
    counter = jnp.arange(column_ids.shape[0], dtype=jnp.int32)
    return jnp.sum(jnp.where(matches, counter[None, None, :], 0), axis=-1)


def strip_table(normal):
    tile_table = lax.all_gather(normal, "pcol", axis=0, tiled=True)
    column_ids = jnp.arange(tile_table.shape[0], dtype=jnp.int32)
    return (tile_table, column_ids)


def multiply(
    tile_table, column_ids, in_pattern, out_pattern, whole_cols, panel_at, row_index, block_share
):
    panel_cols = whole_cols.shape[0]
    named_refs = lax.dynamic_slice_in_dim(in_pattern, panel_at * panel_cols, panel_cols, 0)
    positions = locate(column_ids, named_refs)
    block_rows = lax.dynamic_slice_in_dim(in_pattern, row_index * block_share, block_share, 1)
    table_rows = block_rows[jnp.clip(column_ids, 0, block_rows.shape[0] - 1)]
    needed = tile_table[positions]
    needed_rows = table_rows[positions]
    wanted = lax.dynamic_slice(
        out_pattern, (panel_at * panel_cols, row_index * block_share), (panel_cols, block_share)
    )
    weights = (needed_rows[:, None, :, :] == wanted[:, :, None, None]).astype(jnp.float32)
    selected_entries = jnp.einsum(
        "jtks,jksab->jtkab", weights, needed, precision=lax.Precision.HIGHEST
    )
    return jnp.einsum(
        "jtkab,jkbc->jtac", selected_entries, whole_cols, precision=lax.Precision.HIGHEST
    )


def local(match_tiles, pattern, kept, panel_order):
    panel_cols = match_tiles.shape[0]
    block_share = match_tiles.shape[1]
    row_index = lax.axis_index("prow")
    col_index = lax.axis_index("pcol")
    target = panel_order[col_index]
    whole_cols, normal = gather_pieces_together(match_tiles, True)
    tile_table, column_ids = strip_table(normal)
    product = multiply(
        tile_table, column_ids, pattern, kept, whole_cols, col_index, row_index, block_share
    )
    inflated = product * product
    unused_cols, normal = gather_pieces_together(inflated, False)
    tile_table, column_ids = strip_table(normal)
    target_ids = target * panel_cols + jnp.arange(panel_cols, dtype=jnp.int32)
    target_tiles = tile_table[locate(column_ids, target_ids[None, :])[0]]
    whole_cols = lax.all_gather(target_tiles, "prow", axis=1, tiled=True)
    product = multiply(
        tile_table, column_ids, kept, kept, whole_cols, target, row_index, block_share
    )
    inflated = product * product
    totals = lax.psum(column_partial(inflated), "prow")
    return inflated / totals[:, None, None, :]


def solution(mesh):
    in_specs = (P("pcol", "prow", None, None), P(), P(), P())
    out_specs = P("pcol", "prow", None, None)
    return jax.shard_map(local, mesh=mesh, in_specs=in_specs, out_specs=out_specs, check_vma=False)
```

profile of v0, /device:TPU:0, one launch (start us, length us, event | category | flops | bytes accessed | tf_op | source)
XLA Modules:
  0.0 259.2 jit_solution(4242611748056995517)
XLA Ops:
  6.5 1.1 reduce_sum.78
  7.6 9.5 %all_to_all.15 = f32[4,4,128]{2,1,0:T(4,128)S(1)} all-to-all(f32[4,4,128]{2,1,0:T(4,128)S(1)} %broadcast_in_dim.26), channel_id=1, replica_groups=mesh['prow'=4,'pcol'=32] {'prow'}, dimensions={0} | all-to-all | bytes 16384 | tf_op jit(solution)/shard_map/all_to_all | solution.py:9
  17.2 1.9 broadcast_divide_fusion.2
  19.1 2.6 %broadcast_in_dim.28 = f32[4,4,2,128,128]{4,3,2,1,0:T(8,128)} broadcast(f32[4,2,128,128]{3,2,1,0:T(8,128)} %broadcast_divide_fusion.2), dimensions={1,2,3,4} | broadcast | bytes 2621440 | tf_op jit(solution)/shard_map/broadcast_in_dim | solution.py:9
  21.8 3.6 %all-to-all-start.1 = ((f32[4,4,2,128,128]{4,3,2,1,0:T(8,128)}), f32[4,4,2,128,128]{4,3,2,1,0:T(8,128)S(1)}, u32[]{:S(2)}, u32[]{:S(2)}) async-start(f32[4,4,2,128,128]{4,3,2,1,0:T(8,128)} %broadcast_in_dim.28), calls=%async_computation.1 | async-start | bytes 4194304 | tf_op jit(solution)/shard_map/all_to_all | solution.py:9
  25.5 0.6 dynamic_slice.24
  27.5 0.6 gather_fusion.1
  28.8 21.8 %all-to-all-done.1 = f32[4,4,2,128,128]{4,3,2,1,0:T(8,128)S(1)} async-done(((f32[4,4,2,128,128]{4,3,2,1,0:T(8,128)}), f32[4,4,2,128,128]{4,3,2,1,0:T(8,128)S(1)}, u32[]{:S(2)}, u32[]{:S(2)}) %all-to-all-start.1) | async-done | bytes 2097184 | tf_op jit(solution)/shard_map/all_to_all | solution.py:9
  50.5 1.5 copy.32
  52.0 40.5 %all-gather.5.cloned.1.call-done = f32[128,2,128,128]{3,2,1,0:T(8,128)} async-done(((f32[4,2,128,128]{3,2,1,0:T(8,128)}), f32[128,2,128,128]{3,2,1,0:T(8,128)}) %all-gather.5.cloned.1.call-update) | async-done | bytes 16777232 | tf_op jit(solution)/shard_map/all_gather | solution.py:53
  92.5 8.5 %gather_fusion = f32[32,2,128,128]{3,2,1,0:T(8,128)} fusion(f32[128,2,128,128]{3,2,1,0:T(8,128)} %all-gather.5.cloned.1.call-done, s32[1024]{0:T(1024)S(1)} %pad_clamp_fusion.3), kind=kCustom, calls=%fused_computation | custom fusion | bytes 8388736 | tf_op jit(solution)/shard_map/gather | solution.py:66
  101.0 13.6 %fusion.8 = f32[4,2,8,128,128]{4,1,3,2,0:T(2,128)S(1)} fusion(f32[4,8,2,128,128]{4,3,2,1,0:T(8,128)} %bitcast.61, s32[4,2]{1,0:T(4,128)S(1)} %copy.30, s32[4,8,2]{2,1,0:T(8,128)S(1)} %bitcast.65), kind=kOutput, calls=%fused_computation.15 | convolution fusion | flops 25165952 | bytes 8388896 | tf_op jit(solution)/shard_map/jtks,jksab->jtkab/dot_general | solution.py:72
  114.6 3.8 %fusion.42 = (f32[4,128]{1,0:T(4,128)S(1)}, f32[4,2,128,128]{3,2,1,0:T(8,128)S(1)}) fusion(f32[4,8,128,128,1]{3,2,1,4,0:T(8,128)S(1)} %bitcast.64, f32[4,2,8,128,128]{4,1,3,2,0:T(2,128)S(1)} %fusion.8), kind=kOutput, calls=%fused_computation.55 | convolution fusion | flops 1610874368 | bytes 6817792 | tf_op jit(solution)/shard_map/jtkab,jkbc->jtac/dot_general | solution.py:75
  118.4 9.4 %all_to_all.16 = f32[4,4,128]{2,1,0:T(4,128)S(1)} all-to-all(f32[4,4,128]{2,1,0:T(4,128)S(1)} %broadcast_in_dim.29), channel_id=1, replica_groups=mesh['prow'=4,'pcol'=32] {'prow'}, dimensions={0} | all-to-all | bytes 16384 | tf_op jit(solution)/shard_map/all_to_all | solution.py:9
  127.8 0.8 broadcast_divide_fusion.1
  129.1 70.0 %all-gather.7.cloned.1.call-done = f32[128,2,128,128]{3,2,1,0:T(8,128)} async-done(((f32[4,2,128,128]{3,2,1,0:T(8,128)}), f32[128,2,128,128]{3,2,1,0:T(8,128)}) %all-gather.7.cloned.1.call-update) | async-done | bytes 16777232 | tf_op jit(solution)/shard_map/all_gather | solution.py:53
  199.1 7.1 %gather_fusion.6 = f32[4,2,128,128]{3,2,1,0:T(8,128)} fusion(f32[128,2,128,128]{3,2,1,0:T(8,128)} %all-gather.7.cloned.1.call-done, s32[1024]{0:T(1024)S(1)} %pad_clamp_fusion), kind=kCustom, calls=%fused_computation.6 | custom fusion | bytes 1048592 | tf_op jit(solution)/shard_map/gather | solution.py:95
  206.9 0.6 gather_fusion.4
  208.2 8.5 %gather_fusion.3 = f32[32,2,128,128]{3,2,1,0:T(8,128)} fusion(f32[128,2,128,128]{3,2,1,0:T(8,128)} %all-gather.7.cloned.1.call-done, s32[1024]{0:T(1024)S(1)} %pad_clamp_fusion.1), kind=kCustom, calls=%fused_computation.3 | custom fusion | bytes 8388736 | tf_op jit(solution)/shard_map/gather | solution.py:66
  216.7 14.7 %fusion.11 = f32[4,2,8,128,128]{4,1,3,2,0:T(2,128)} fusion(f32[4,8,2,128,128]{4,3,2,1,0:T(8,128)} %bitcast.62, s32[4,2]{1,0:T(4,128)S(1)} %copy.38, s32[4,8,2]{2,1,0:T(8,128)S(1)} %bitcast.66), kind=kOutput, calls=%fused_computation.16 | convolution fusion | flops 25165952 | bytes 8388896 | tf_op jit(solution)/shard_map/jtks,jksab->jtkab/dot_general | solution.py:72
  231.4 5.2 %all-gather.9.cloned.1.call-done = f32[4,8,128,128]{3,2,1,0:T(8,128)} async-done(((f32[4,2,128,128]{3,2,1,0:T(8,128)}), f32[4,8,128,128]{3,2,1,0:T(8,128)}) %all-gather.9.cloned.1.call-update) | async-done | bytes 2097168 | tf_op jit(solution)/shard_map/all_gather | solution.py:96
  236.6 6.7 %fusion.43 = (f32[4,128]{1,0:T(4,128)S(1)}, f32[4,2,128,128]{3,2,1,0:T(8,128)S(1)}) fusion(f32[4,8,128,128]{3,2,1,0:T(8,128)} %all-gather.9.cloned.1.call-done, f32[4,2,8,128,128]{4,1,3,2,0:T(2,128)} %fusion.11), kind=kOutput, calls=%fused_computation.56 | convolution fusion | flops 1610874368 | bytes 6817792 | tf_op jit(solution)/shard_map/jtkab,jkbc->jtac/dot_general | solution.py:75
  243.3 8.6 %psum.7 = f32[4,128]{1,0:T(4,128)S(1)} all-reduce(f32[4,128]{1,0:T(4,128)S(1)} %get-tuple-element.9), channel_id=1, replica_groups=mesh['prow'=4,'pcol'=32] {'prow'}, use_global_device_ids=true, to_apply=%region_8.9 | all-reduce | flops 512 | bytes 4096 | tf_op jit(solution)/shard_map/psum | solution.py:101
  251.9 0.8 broadcast_divide_fusion
  (44 shorter events, 3.2 us)
Async XLA Ops:
  6.5 85.9 %all-gather.5.cloned.1.call-start = ((), (), s32[]{:S(2)}) async-start(), calls=%async_computation.3 | async-start | bytes 17301504 | tf_op jit(solution)/shard_map/all_gather | solution.py:53
  17.2 8.3 %copy-start.3 = (s32[32]{0:T(128)S(1)}, s32[32]{0:T(128)}, u32[]{:S(2)}) copy-start(s32[32]{0:T(128)} %param.7) | copy-start | bytes 388
  17.2 9.5 %copy-start.1 = (s32[128,8]{0,1:T(8,128)S(1)}, s32[128,8]{0,1:T(8,128)}, u32[]{:S(2)}) copy-start(s32[128,8]{0,1:T(8,128)} %param.6) | copy-start | bytes 12292
  17.2 9.7 %copy-start.2 = (s32[128,8]{0,1:T(8,128)S(1)}, s32[128,8]{0,1:T(8,128)}, u32[]{:S(2)}) copy-start(s32[128,8]{0,1:T(8,128)} %param.5) | copy-start | bytes 12292
  21.8 28.8 %all-to-all-start.1 = ((f32[4,4,2,128,128]{4,3,2,1,0:T(8,128)}), f32[4,4,2,128,128]{4,3,2,1,0:T(8,128)S(1)}, u32[]{:S(2)}, u32[]{:S(2)}) async-start(f32[4,4,2,128,128]{4,3,2,1,0:T(8,128)} %broadcast_in_dim.28), calls=%async_computation.1 | async-start | bytes 4194304 | tf_op jit(solution)/shard_map/all_to_all | solution.py:9
  25.4 173.7 %all-gather.7.cloned.1.call-start = ((), (), s32[]{:S(2)}) async-start(), calls=%async_computation.4 | async-start | bytes 17301504 | tf_op jit(solution)/shard_map/all_gather | solution.py:53
  101.0 13.6 %copy-start = (f32[4,4,2,128,128]{4,3,2,1,0:T(8,128)S(1)}, f32[4,4,2,128,128]{4,3,2,1,0:T(8,128)}, u32[]{:S(2)}) copy-start(f32[4,4,2,128,128]{4,3,2,1,0:T(8,128)} %copy.32) | copy-start | bytes 6291460
  128.7 107.9 %all-gather.9.cloned.1.call-start = ((), (), s32[]{:S(2)}) async-start(), calls=%async_computation.5 | async-start | bytes 2621440 | tf_op jit(solution)/shard_map/all_gather | solution.py:96
Sparse Core Ops, SparseCore 0:
  19.2 73.1 all-gather.4
  128.8 70.2 all-gather.6
  206.4 30.1 all-gather.8
where the time goes:
time: 260 us; the launch traced here: 259 us
  waiting for transfers between devices  137 us (53%)
  matrix products  38.9 us (15%)
  local copies, waits for them, and re-layouts  32.3 us (12%)
  blocking collectives  27.5 us (11%)
  between operations  13.9 us (5%)
  other arithmetic  5.37 us (2%)
  starting transfers between devices  3.87 us (1%)
    all_gather x2, waiting for transfers between devices, strip_table(): tile_table = lax.all_gather(normal, 'pcol', axis=0, tiled=True)  110 us
    dot_general x2, matrix products, multiply(): jnp.einsum('jtks,jksab->jtkab', weights, needed, precision=lax.Precision....  28.3 us
    all_to_all x1, waiting for transfers between devices, copy_for_each(): lax.all_to_all(jnp.broadcast_to(x[None], (length, *x.shape)), axis, 0, 0,...  21.8 us
    all_to_all x2, blocking collectives, copy_for_each(): lax.all_to_all(jnp.broadcast_to(x[None], (length, *x.shape)), axis, 0, 0,...  18.9 us
    gather x2, local copies, waits for them, and re-layouts, multiply(): needed = tile_table[positions]  17 us
    dot_general x2, matrix products, multiply(): jnp.einsum('jtkab,jkbc->jtac', selected_entries, whole_cols, precision=la...  10.5 us
    psum x1, blocking collectives, local(): totals = lax.psum(column_partial(inflated), 'prow')  8.59 us
    gather x1, local copies, waits for them, and re-layouts, local(): target_tiles = tile_table[locate(column_ids, target_ids[None, :])[0]]  7.14 us
  transfers between devices with their start and end apart: 4, of which 4 were waited for; matrix products, arithmetic and copies ran while one was open for 12% of the time, Pallas kernels for 0%

commit v1 on v0

--- a/solution.py
+++ b/solution.py
@@ -2,6 +2,11 @@
 import jax.numpy as jnp
 from jax import lax
 from jax.sharding import PartitionSpec as P
+
+
+def gather_from_all(x, axis, dim):
+    copies = jnp.concatenate([x] * lax.axis_size(axis), axis=dim)
+    return lax.all_to_all(copies, axis, dim, dim, tiled=True)
 
 
 def copy_for_each(x, axis):
@@ -50,7 +55,7 @@
 
 
 def strip_table(normal):
-    tile_table = lax.all_gather(normal, "pcol", axis=0, tiled=True)
+    tile_table = gather_from_all(normal, "pcol", 0)
     column_ids = jnp.arange(tile_table.shape[0], dtype=jnp.int32)
     return (tile_table, column_ids)
 

time: 260 us -> 622 us (2.39)
  waiting for transfers between devices: 137 us -> 435 us
  other arithmetic: 5.37 us -> 31.8 us
  local copies, waits for them, and re-layouts: 32.3 us -> 58 us
  starting transfers between devices: 3.87 us -> 17.5 us
    all_to_all x0 -> x2, waiting for transfers between devices: none -> 421 us  [gather_from_all(): return lax.all_to_all(copies, axis, dim, dim, tiled=True)]
    all_gather x2 -> x0, waiting for transfers between devices: 110 us -> none  [strip_table(): tile_table = lax.all_gather(normal, 'pcol', axis=0, tiled=True)]
    unnamed x0 -> x32, other arithmetic: none -> 28.3 us
    unnamed x10 -> x40, local copies, waits for them, and re-layouts: 0.25 us -> 25.6 us
    all_to_all x0 -> x2, starting transfers between devices: none -> 13.8 us  [gather_from_all(): return lax.all_to_all(copies, axis, dim, dim, tiled=True)]
    all_to_all x1, waiting for transfers between devices: 21.8 us -> 14.2 us  [copy_for_each(): lax.all_to_all(jnp.broadcast_to(x[None], (length, *x.shape)), axis, 0, 0,...]
  transfers between devices with their start and end apart: 4 -> 4, of which waited for: 4 -> 4; matrix products, arithmetic and copies ran while one was open for 12% -> 7% of each run, Pallas kernels for 0% -> 0%
where the time goes in v1:
time: 622 us; the launch traced here: 621 us
  waiting for transfers between devices  435 us (70%)
  local copies, waits for them, and re-layouts  58 us (9%)
  matrix products  38.8 us (6%)
  other arithmetic  31.8 us (5%)
  blocking collectives  25.8 us (4%)
  starting transfers between devices  17.5 us (3%)
  between operations  14.2 us (2%)
    all_to_all x2, waiting for transfers between devices, gather_from_all(): return lax.all_to_all(copies, axis, dim, dim, tiled=True)  421 us
    unnamed x32, other arithmetic  28.3 us
    dot_general x2, matrix products, multiply(): jnp.einsum('jtks,jksab->jtkab', weights, needed, precision=lax.Precision....  28.2 us
    unnamed x40, local copies, waits for them, and re-layouts  25.6 us
    gather x2, local copies, waits for them, and re-layouts, multiply(): needed = tile_table[positions]  17.5 us
    all_to_all x2, blocking collectives, copy_for_each(): lax.all_to_all(jnp.broadcast_to(x[None], (length, *x.shape)), axis, 0, 0,...  17.2 us
    all_to_all x1, waiting for transfers between devices, copy_for_each(): lax.all_to_all(jnp.broadcast_to(x[None], (length, *x.shape)), axis, 0, 0,...  14.2 us
    all_to_all x2, starting transfers between devices, gather_from_all(): return lax.all_to_all(copies, axis, dim, dim, tiled=True)  13.8 us
  transfers between devices with their start and end apart: 4, of which 4 were waited for; matrix products, arithmetic and copies ran while one was open for 7% of the time, Pallas kernels for 0%

profile of v1, /device:TPU:0, one launch (start us, length us, event | category | flops | bytes accessed | tf_op | source)
XLA Modules:
  0.0 621.3 jit_solution(6101463635285976835)
XLA Ops:
  6.5 1.1 reduce_sum.78
  7.6 9.5 %all_to_all.25 = f32[4,4,128]{2,1,0:T(4,128)S(1)} all-to-all(f32[4,4,128]{2,1,0:T(4,128)S(1)} %broadcast_in_dim.26), channel_id=1, replica_groups=mesh['prow'=4,'pcol'=32] {'prow'}, dimensions={0} | all-to-all | bytes 16384 | tf_op jit(solution)/shard_map/all_to_all | solution.py:14
  17.2 1.9 constant_dynamic-update-slice_fusion.31
  32.7 0.9 constant_dynamic-update-slice_fusion.14
  34.4 1.6 broadcast_in_dim.28
  36.0 3.6 all-to-all-start.2
  50.6 14.2 %all-to-all-done.2 = f32[4,4,2,128,128]{4,3,2,1,0:T(8,128)S(1)} async-done(((f32[4,4,2,128,128]{4,3,2,1,0:T(8,128)}), f32[4,4,2,128,128]{4,3,2,1,0:T(8,128)S(1)}, u32[]{:S(2)}, u32[]{:S(2)}) %all-to-all-start.2) | async-done | bytes 2097184 | tf_op jit(solution)/shard_map/all_to_all | solution.py:14
  64.7 8.6 %all-to-all-start.1 = ((f32[128,2,128,128]{3,2,1,0:T(8,128)}), f32[128,2,128,128]{3,2,1,0:T(8,128)}, u32[]{:S(2)}, u32[]{:S(2)}) async-start(f32[128,2,128,128]{3,2,1,0:T(8,128)} %constant_dynamic-update-slice_fusion), calls=%async_computation.1 | async-start | bytes 33554432 | tf_op jit(solution)/shard_map/all_to_all | solution.py:9
  76.7 1.5 copy.32
  78.1 208.3 %all-to-all-done.1 = f32[128,2,128,128]{3,2,1,0:T(8,128)} async-done(((f32[128,2,128,128]{3,2,1,0:T(8,128)}), f32[128,2,128,128]{3,2,1,0:T(8,128)}, u32[]{:S(2)}, u32[]{:S(2)}) %all-to-all-start.1) | async-done | bytes 16777248 | tf_op jit(solution)/shard_map/all_to_all | solution.py:9
  286.5 8.5 %gather_fusion = f32[32,2,128,128]{3,2,1,0:T(8,128)} fusion(f32[128,2,128,128]{3,2,1,0:T(8,128)} %all-to-all-done.1, s32[1024]{0:T(1024)S(1)} %pad_clamp_fusion.3), kind=kCustom, calls=%fused_computation | custom fusion | bytes 8388736 | tf_op jit(solution)/shard_map/gather | solution.py:71
  295.0 13.5 %fusion.8 = f32[4,2,8,128,128]{4,1,3,2,0:T(2,128)S(1)} fusion(f32[4,8,2,128,128]{4,3,2,1,0:T(8,128)} %bitcast.61, s32[4,2]{1,0:T(4,128)S(1)} %copy.30, s32[4,8,2]{2,1,0:T(8,128)S(1)} %bitcast.65), kind=kOutput, calls=%fused_computation.15 | convolution fusion | flops 25165952 | bytes 8388896 | tf_op jit(solution)/shard_map/jtks,jksab->jtkab/dot_general | solution.py:77
  308.4 3.9 fusion.42
  312.3 7.7 %all_to_all.26 = f32[4,4,128]{2,1,0:T(4,128)S(1)} all-to-all(f32[4,4,128]{2,1,0:T(4,128)S(1)} %broadcast_in_dim.29), channel_id=1, replica_groups=mesh['prow'=4,'pcol'=32] {'prow'}, dimensions={0} | all-to-all | bytes 16384 | tf_op jit(solution)/shard_map/all_to_all | solution.py:14
  333.6 0.9 constant_dynamic-update-slice_fusion.47
  334.5 0.9 constant_dynamic-update-slice_fusion.46
  341.3 0.9 constant_dynamic-update-slice_fusion.38
  347.2 5.2 all-to-all-start.4
  353.1 212.6 %all-to-all-done.4 = f32[128,2,128,128]{3,2,1,0:T(8,128)} async-done(((f32[128,2,128,128]{3,2,1,0:T(8,128)}), f32[128,2,128,128]{3,2,1,0:T(8,128)}, u32[]{:S(2)}, u32[]{:S(2)}) %all-to-all-start.4) | async-done | bytes 16777248 | tf_op jit(solution)/shard_map/all_to_all | solution.py:9
  565.7 7.1 %gather_fusion.6 = f32[4,2,128,128]{3,2,1,0:T(8,128)} fusion(f32[128,2,128,128]{3,2,1,0:T(8,128)} %all-to-all-done.4, s32[1024]{0:T(1024)S(1)} %get-tuple-element.15), kind=kCustom, calls=%fused_computation.6 | custom fusion | bytes 1048592 | tf_op jit(solution)/shard_map/gather | solution.py:100
  574.3 9.0 %gather_fusion.3 = f32[32,2,128,128]{3,2,1,0:T(8,128)} fusion(f32[128,2,128,128]{3,2,1,0:T(8,128)} %all-to-all-done.4, s32[1024]{0:T(1024)S(1)} %get-tuple-element.16), kind=kCustom, calls=%fused_computation.3 | custom fusion | bytes 8388736 | tf_op jit(solution)/shard_map/gather | solution.py:71
  583.3 14.8 %fusion.11 = f32[4,2,8,128,128]{4,1,3,2,0:T(2,128)} fusion(f32[4,8,2,128,128]{4,3,2,1,0:T(8,128)} %bitcast.62, s32[4,2]{1,0:T(4,128)S(1)} %copy.38, s32[4,8,2]{2,1,0:T(8,128)S(1)} %bitcast.66), kind=kOutput, calls=%fused_computation.16 | convolution fusion | flops 25165952 | bytes 8388896 | tf_op jit(solution)/shard_map/jtks,jksab->jtkab/dot_general | solution.py:77
  598.3 6.7 %fusion.43 = (f32[4,128]{1,0:T(4,128)S(1)}, f32[4,2,128,128]{3,2,1,0:T(8,128)S(1)}) fusion(f32[4,8,128,128]{3,2,1,0:T(8,128)} %all-gather.3.cloned.1.call-done, f32[4,2,8,128,128]{4,1,3,2,0:T(2,128)} %fusion.11), kind=kOutput, calls=%fused_computation.120 | convolution fusion | flops 1610874368 | bytes 6817792 | tf_op jit(solution)/shard_map/jtkab,jkbc->jtac/dot_general | solution.py:80
  605.0 8.6 %psum.7 = f32[4,128]{1,0:T(4,128)S(1)} all-reduce(f32[4,128]{1,0:T(4,128)S(1)} %get-tuple-element.11), channel_id=1, replica_groups=mesh['prow'=4,'pcol'=32] {'prow'}, use_global_device_ids=true, to_apply=%region_8.9 | all-reduce | flops 512 | bytes 4096 | tf_op jit(solution)/shard_map/psum | solution.py:106
  (103 shorter events, 55.7 us)
Async XLA Ops:
  36.0 28.8 %all-to-all-start.2 = ((f32[4,4,2,128,128]{4,3,2,1,0:T(8,128)}), f32[4,4,2,128,128]{4,3,2,1,0:T(8,128)S(1)}, u32[]{:S(2)}, u32[]{:S(2)}) async-start(f32[4,4,2,128,128]{4,3,2,1,0:T(8,128)} %broadcast_in_dim.28), calls=%async_computation.2 | async-start | bytes 4194304 | tf_op jit(solution)/shard_map/all_to_all | solution.py:14
  50.5 22.8 %copy-start.3 = (s32[32]{0:T(128)S(1)}, s32[32]{0:T(128)}, u32[]{:S(2)}) copy-start(s32[32]{0:T(128)} %param.7) | copy-start | bytes 388
  50.6 24.1 %copy-start.2 = (s32[128,8]{0,1:T(8,128)S(1)}, s32[128,8]{0,1:T(8,128)}, u32[]{:S(2)}) copy-start(s32[128,8]{0,1:T(8,128)} %param.5) | copy-start | bytes 12292
  50.6 24.6 %copy-start.1 = (s32[128,8]{0,1:T(8,128)S(1)}, s32[128,8]{0,1:T(8,128)}, u32[]{:S(2)}) copy-start(s32[128,8]{0,1:T(8,128)} %param.6) | copy-start | bytes 12292
  64.7 221.7 %all-to-all-start.1 = ((f32[128,2,128,128]{3,2,1,0:T(8,128)}), f32[128,2,128,128]{3,2,1,0:T(8,128)}, u32[]{:S(2)}, u32[]{:S(2)}) async-start(f32[128,2,128,128]{3,2,1,0:T(8,128)} %constant_dynamic-update-slice_fusion), calls=%async_computation.1 | async-start | bytes 33554432 | tf_op jit(solution)/shard_map/all_to_all | solution.py:9
  78.1 230.3 %copy-start = (f32[4,4,2,128,128]{4,3,2,1,0:T(8,128)S(1)}, f32[4,4,2,128,128]{4,3,2,1,0:T(8,128)}, u32[]{:S(2)}) copy-start(f32[4,4,2,128,128]{4,3,2,1,0:T(8,128)} %copy.32) | copy-start | bytes 6291460
  347.2 218.5 %all-to-all-start.4 = ((f32[128,2,128,128]{3,2,1,0:T(8,128)}), f32[128,2,128,128]{3,2,1,0:T(8,128)}, u32[]{:S(2)}, u32[]{:S(2)}) async-start(f32[128,2,128,128]{3,2,1,0:T(8,128)} %constant_dynamic-update-slice_fusion.32), calls=%async_computation.4 | async-start | bytes 33554432 | tf_op jit(solution)/shard_map/all_to_all | solution.py:9
  352.4 245.9 %all-gather.3.cloned.1.call-start = ((), (), s32[]{:S(2)}) async-start(), calls=%async_computation.5 | async-start | bytes 2621440 | tf_op jit(solution)/shard_map/all_gather | solution.py:101
Sparse Core Ops, SparseCore 0:
  573.0 25.2 all-gather.2
